TPU v7x, 512 devices: a 4x2x32 block of a 4x8x32 slice. The times are simulated.
512 devices in a mesh: groups: 2 (over y), sky: 32 (over z), epoch: 4 (over x), band: 2 (over core).
Axes of the slice: x: 4, y: 2, z: 32, core: 2. Of those that a mesh axis runs over, the one named last changes fastest.
The devices are a block of a 4x8x32 slice.
Arguments:
- slot_pixels: bfloat16 [12288, 6, 32, 512], P(('groups', 'sky', 'epoch'), 'band'), parts along dimension 0, may hold values from -6 to 6
- slot_tile: int32 [12288, 1], P(('groups', 'sky', 'epoch')), parts along dimension 0, may hold values from 0 to 31; in each aligned block of 48 rows (0 to 47, 48 to 95, ...) at most 2 rows name the same one
- slot_offset: int32 [12288, 2], P(('groups', 'sky', 'epoch')), parts along dimension 0, may hold values from -5 to 5
- slot_frac: bfloat16 [12288, 2], P(('groups', 'sky', 'epoch')), parts along dimension 0, may hold values from 0.049804688 to 0.94921875
- slot_sigma: bfloat16 [12288, 6], P(('groups', 'sky', 'epoch'), 'band'), parts along dimension 0, may hold values from 0.5 to 2
- clip_mask: int32 [12288, 6, 16], P(('groups', 'sky', 'epoch')), parts along dimension 0, may hold values 0 or 1
- slot_count: int32 [256], P(('groups', 'sky', 'epoch')), parts along dimension 0, may hold values from 36 to 48
- template: bfloat16 [6, 2048, 512], P('band', ('groups', 'sky')), parts along dimension 1, may hold values from -6 to 6
- prior_weight: float32 [6, 2048], P('band', ('groups', 'sky')), parts along dimension 1, may hold values from 0.5 to 4
Outputs:
- coadd_image: bfloat16 [6, 2048, 512], P('band', ('groups', 'sky'), 'epoch'), parts along dimension 1
- depth_norm: bfloat16 [6, 2048, 512], P('band', ('groups', 'sky'), 'epoch'), parts along dimension 1
There are 2 independent parts, one for each index of `groups`. A program takes and returns all parts, laid end to end along the dimension named above; each array names one. Nothing has to cross between parts.
Inputs may be any that keep to these rules, and one draw needn't show every extreme that they name: `slot_tile`: among the 48 rows of one reading device no owner is named more than 2 times, a bound that some block reaches. `slot_count`: slots of a reading device at or after its count are padding.
All inputs are finite; a program needn't handle non-finite values. No bound on the sum of `clip_mask` on one device may be relied on, other than what follows from the above.
Results may differ from a plain program's by a relative error of at most 0.014.
Values may be sent and summed in bfloat16 or wider, within the bound.
A program may use at most 64 MiB of HBM per device.

v0:
```python
import functools
import math

import jax
import jax.numpy as jnp
from jax import lax
from jax.sharding import PartitionSpec as P

ROWS_DEV = 32
MARGIN = 8
CAPACITY = 2


CLIP_WIDTH = 3.0


def split_up(shard, dim, size):
    lengths = shard.shape
    parts = shard.reshape(*lengths[:dim], size, lengths[dim] // size, *lengths[dim + 1 :])
    return jnp.moveaxis(parts, dim, 0)


def summed_on_arrival(shard, axis, dim):
    parts = split_up(shard, dim, lax.axis_size(axis))
    arrived = lax.all_to_all(parts, axis, split_axis=0, concat_axis=0, tiled=True)
    return arrived.astype(jnp.float32).sum(axis=0)


def padded(cells, sides, width):
    for axis, dim in sides:
        count = lax.axis_size(axis)
        ends = count - 1
        head = lax.slice_in_dim(cells, 0, width, axis=dim)
        tail = lax.slice_in_dim(cells, cells.shape[dim] - width, cells.shape[dim], axis=dim)
        cells = jnp.concatenate(
            [
                lax.ppermute(tail, axis, [(i, (i + 1) % count) for i in range(ends)]),
                cells,
                lax.ppermute(head, axis, [((i + 1) % count, i) for i in range(ends)]),
            ],
            axis=dim,
        )
    return cells


def side_by_side(arrays, axis, split_dim, concat_dim, along):
    ends, at = ([], 0)
    for a in arrays[:-1]:
        at += a.shape[along]
        ends.append(at)
    both = jnp.concatenate(arrays, axis=along)
    return tuple(
        jnp.split(
            lax.all_to_all(both, axis, split_axis=split_dim, concat_axis=concat_dim, tiled=True),
            ends,
            axis=along,
        )
    )


def one_axis_at_a_time(shard, axes):
    return functools.reduce(lax.psum, axes, shard)


def lanczos(distance):
    inside = jnp.abs(distance) < 3.0
    return jnp.where(inside, jnp.sinc(distance) * jnp.sinc(distance / 3.0), 0.0)


def warp_table(shifts, fractions, length_out, length_in, margin_rows):
    out_index = lax.broadcasted_iota(jnp.int32, (1, length_out, length_in), 1)
    in_index = lax.broadcasted_iota(jnp.int32, (1, length_out, length_in), 2)
    gap_index = out_index - margin_rows - shifts[:, None, None] - in_index
    distance = gap_index.astype(jnp.float32) - fractions[:, None, None]
    return lanczos(distance).astype(jnp.bfloat16)


def warp_columns(pixels, shifts, fractions):
    tile_cols = pixels.shape[3]
    kernel_table = warp_table(shifts, fractions, tile_cols, tile_cols, 0)
    warped = jnp.einsum("sbrk,sjk->sbrj", pixels, kernel_table, preferred_element_type=jnp.float32)
    return warped.astype(jnp.bfloat16)


def column_cover(shifts, fractions, tile_cols):
    column_index = lax.broadcasted_iota(jnp.int32, (1, tile_cols), 1)
    cover = jnp.zeros((shifts.shape[0], tile_cols), jnp.float32)
    for step_back in range(-3, 3):
        rounded = lanczos(jnp.float32(-step_back) - fractions).astype(jnp.bfloat16)
        weight_tap = lax.optimization_barrier(rounded).astype(jnp.float32)
        source_col = column_index - shifts[:, None] + step_back
        inside = (source_col >= 0) & (source_col < tile_cols)
        cover = cover + jnp.where(inside, weight_tap[:, None], 0.0)
    return jnp.clip(cover, 0.0, 1.0)


def epoch_sum(totals):
    return summed_on_arrival(totals.astype(jnp.bfloat16), "epoch", 3)


def add_seams(totals):
    rims = jnp.concatenate([totals[:, :, :MARGIN], totals[:, :, -MARGIN:]], 2)
    framed_rims = padded(rims.astype(jnp.bfloat16), (("sky", 2),), MARGIN).astype(rims.dtype)
    own_rows = totals[:, :, MARGIN : MARGIN + ROWS_DEV]
    own_rows = own_rows.at[:, :, :MARGIN].add(framed_rims[:, :, :MARGIN])
    own_rows = own_rows.at[:, :, ROWS_DEV - MARGIN :].add(framed_rims[:, :, 3 * MARGIN :])
    return own_rows


def on_device(
    slot_pixels,
    slot_tile,
    slot_offset,
    slot_frac,
    slot_sigma,
    clip_mask,
    slot_count,
    template,
    prior_weight,
):
    sky_count = lax.axis_size("sky")
    held = slot_pixels.shape[0]
    tile_cols = slot_pixels.shape[3]
    local_bands = slot_pixels.shape[1]
    canvas_rows = ROWS_DEV + 2 * MARGIN
    routes_total = sky_count * CAPACITY
    target = slot_tile[:, 0]
    owners = jnp.arange(sky_count, dtype=jnp.int32)
    onehot = (target[:, None] == owners[None, :]).astype(jnp.int32)
    slot_rank = jnp.sum(jnp.cumsum(onehot, 0) * onehot, 1) - 1
    position = target * CAPACITY + slot_rank
    held_index = jnp.arange(held, dtype=jnp.int32)
    is_live = held_index < slot_count[0]
    chooser = position[None, :] == jnp.arange(routes_total, dtype=jnp.int32)[:, None]
    source = jnp.sum(jnp.where(chooser, held_index[None, :], 0), 1)
    filled = jnp.any(chooser & is_live[None, :], 1).astype(jnp.int32)

    def pack(array):
        taken = jnp.take(array, source, axis=0)
        return taken.reshape((sky_count, CAPACITY) + array.shape[1:])

    packed_mask = pack(clip_mask) * filled.reshape(sky_count, CAPACITY)[:, :, None, None]
    received = (
        lax.all_to_all(pack(slot_pixels), "sky", split_axis=0, concat_axis=0, tiled=True),
        lax.all_to_all(pack(slot_offset), "sky", split_axis=0, concat_axis=0, tiled=True),
        *side_by_side((pack(slot_frac), pack(slot_sigma)), "sky", 0, 0, 2),
        lax.all_to_all(packed_mask, "sky", split_axis=0, concat_axis=0, tiled=True),
    )
    received = tuple((array.reshape((routes_total,) + array.shape[2:]) for array in received))
    framed = padded(template, (("sky", 1),), MARGIN).astype(jnp.float32)

    def accumulate(totals, pieces):
        pixels, offsets, fractions, sigmas, masks = pieces
        fractions = fractions.astype(jnp.float32)
        columns = warp_columns(pixels, offsets[:, 1], fractions[:, 1])
        row_table = warp_table(offsets[:, 0], fractions[:, 0], canvas_rows, ROWS_DEV, MARGIN)
        warped = jnp.einsum(
            "sir,sbrj->sbij", row_table, columns, preferred_element_type=jnp.float32
        )
        row_cover = jnp.clip(jnp.sum(row_table.astype(jnp.float32), 2), 0.0, 1.0)
        col_cover = column_cover(offsets[:, 1], fractions[:, 1], tile_cols)
        block_slots = masks.shape[0]
        block_mask = masks.astype(jnp.float32)
        expanded = jnp.broadcast_to(
            block_mask[:, :, None, :, None], (block_slots, canvas_rows // 8, 8, tile_cols // 32, 32)
        )
        expanded = expanded.reshape(block_slots, canvas_rows, tile_cols)
        plane = expanded * row_cover[:, :, None] * col_cover[:, None, :]
        sigma_values = sigmas.astype(jnp.float32)
        weight = plane[:, None] / (sigma_values * sigma_values)[:, :, None, None]
        scale = CLIP_WIDTH * sigma_values[:, :, None, None]
        clipped = framed[None] + scale * jnp.tanh((warped - framed[None]) / scale)
        flux_part = jnp.sum(weight * clipped, 0)
        weight_part = jnp.sum(weight, 0)
        return (totals + jnp.stack([flux_part, weight_part], 0), None)

    block_slots = math.gcd(8, routes_total)
    blocked = tuple(
        (
            array.reshape((routes_total // block_slots, block_slots) + array.shape[1:])
            for array in received
        )
    )
    initial = jnp.zeros((2, local_bands, canvas_rows, tile_cols), jnp.float32)
    totals, _ = lax.scan(accumulate, initial, blocked)
    own_rows = add_seams(epoch_sum(totals))
    flux_sum = own_rows[0]
    weight_sum = own_rows[1]
    part_width = own_rows.shape[3]
    epoch_position = lax.axis_index("epoch")
    template_part = lax.dynamic_slice_in_dim(
        template, epoch_position * part_width, part_width, 2
    ).astype(jnp.float32)
    prior = prior_weight[:, :, None]
    coadd_image = ((flux_sum + prior * template_part) / (weight_sum + prior)).astype(jnp.bfloat16)
    depth_map = weight_sum + prior
    band_total = one_axis_at_a_time(jnp.sum(depth_map, axis=(1, 2)), ("sky", "epoch"))
    band_mean = band_total / (ROWS_DEV * sky_count * tile_cols)
    depth_norm = (depth_map / band_mean[:, None, None]).astype(jnp.bfloat16)
    return (coadd_image, depth_norm)


def solution(mesh):
    in_specs = (
        P(("groups", "sky", "epoch"), "band", None, None),
        P(("groups", "sky", "epoch"), None),
        P(("groups", "sky", "epoch"), None),
        P(("groups", "sky", "epoch"), None),
        P(("groups", "sky", "epoch"), "band"),
        P(("groups", "sky", "epoch"), None, None),
        P(("groups", "sky", "epoch")),
        P("band", ("groups", "sky"), None),
        P("band", ("groups", "sky")),
    )
    out_specs = (P("band", ("groups", "sky"), "epoch"), P("band", ("groups", "sky"), "epoch"))
    return jax.shard_map(
        on_device, mesh=mesh, in_specs=in_specs, out_specs=out_specs, check_vma=False
    )
```

profile of v0, /device:TPU:40, one launch (start us, length us, event | category | flops | bytes accessed | tf_op | source)
XLA Modules:
  0.0 1011.3 jit_solution(4690587157069409075)
XLA Ops:
  5.5 45.8 %all-to-all-start.1 = ((s32[32,2,2]{1,2,0:T(2,128)}), s32[32,2,2]{1,2,0:T(2,128)S(1)}, u32[]{:S(2)}, u32[]{:S(2)}) async-start(s32[32,2,2]{1,2,0:T(2,128)} %copy.89), calls=%async_computation.1 | async-start | bytes 65536 | tf_op jit(solution)/shard_map/all_to_all | solution.py:145
  58.0 15.7 %all-to-all-done.1 = s32[32,2,2]{1,2,0:T(2,128)S(1)} async-done(((s32[32,2,2]{1,2,0:T(2,128)}), s32[32,2,2]{1,2,0:T(2,128)S(1)}, u32[]{:S(2)}, u32[]{:S(2)}) %all-to-all-start.1) | async-done | bytes 544 | tf_op jit(solution)/shard_map/all_to_all | solution.py:145
  73.8 6.3 all-to-all-start.2
  81.1 5.9 gather_fusion.4
  87.0 14.7 %all-to-all-done.2 = bf16[32,2,5]{2,1,0:T(2,128)(2,1)S(1)} async-done(((bf16[32,2,5]{2,1,0:T(2,128)(2,1)}), bf16[32,2,5]{2,1,0:T(2,128)(2,1)S(1)}, u32[]{:S(2)}, u32[]{:S(2)}) %all-to-all-start.2) | async-done | bytes 672 | tf_op jit(solution)/shard_map/all_to_all | solution.py:54
  101.7 7.3 all-to-all-start
  109.1 6.1 broadcast_select_fusion
  115.2 16.3 %all-to-all-done = s32[32,1,192]{2,1,0:T(1,128)S(1)} async-done(((s32[32,1,192]{2,1,0:T(1,128)}), s32[32,1,192]{2,1,0:T(1,128)S(1)}, u32[]{:S(2)}, u32[]{:S(2)}) %all-to-all-start) | async-done | bytes 24608 | tf_op jit(solution)/shard_map/all_to_all | solution.py:147
  131.5 5.8 all-to-all-start.3
  137.4 3.3 collective-permute-start
  142.4 518.0 %collective-permute-done = bf16[3,8,512]{2,1,0:T(8,128)(2,1)S(1)} collective-permute-done((bf16[3,8,512]{2,1,0:T(8,128)(2,1)S(1)}, bf16[3,8,512]{2,1,0:T(8,128)(2,1)S(1)}, u32[]{:S(2)}, u32[]{:S(2)}) %collective-permute-start) | collective-permute-done | bytes 24608 | tf_op jit(solution)/shard_map/ppermute | solution.py:37
  660.5 12.7 %collective-permute-done.1 = bf16[3,8,512]{2,1,0:T(8,128)(2,1)S(1)} collective-permute-done((bf16[3,8,512]{2,1,0:T(8,128)(2,1)S(1)}, bf16[3,8,512]{2,1,0:T(8,128)(2,1)S(1)}, u32[]{:S(2)}, u32[]{:S(2)}) %collective-permute-start.1) | collective-permute-done | bytes 24608 | tf_op jit(solution)/shard_map/ppermute | solution.py:39
  675.5 3.7 all-to-all-done.3
  679.1 231.2 %while.15 = (s32[]{:T(128)}, f32[2,3,48,512]{3,2,1,0:T(8,128)}, s32[8,8,6,16]{3,1,0,2:T(8,128)S(1)}, s32[8,8,2]{1,0,2:T(8,128)S(1)}, bf16[8,8,2]{1,2,0:T(2,128)(...) while((s32[]{:T(128)}, f32[2,3,48,512]{3,2,1,0:T(8,128)}, ...), condition=%wide.region_8.12_spmd.clone, body=%wide.region_4.11_spmd.clone.sunk | while | flops 606097728 | bytes 13722023 | solution.py:185
  680.2 2.1 reshape.369
  683.7 23.0 %fusion.228 = f32[3,48,512]{2,1,0:T(8,128)S(1)} fusion(f32[8,3]{1,0:T(8,128)S(1)} %copy.121, f32[3,48,512]{2,1,0:T(8,128)} %get-tuple-element.331, f32[8,3]{1,0:T(8,128)S(1)} %copy.120, f32[8,48,512]{2,1,0:T(8,128)S(1)} %multiply_multiply_fusion.30, f32[8]{0:T(128)S(1)} %get-tuple-element.304, s32[8]{0:T(128)S(1)} %get-tuple-element.300, ...), kind=kOutput, calls=%fused_computation.69.clone.1 | convolution fusion | flops 603058176 | bytes 2163712 | tf_op jit(solution)/shard_map/while/body/eval_jaxpr/sir,sbrj->sbij/dot_general | solution.py:157
  709.1 2.1 reshape.369
  712.6 23.0 %fusion.228 = f32[3,48,512]{2,1,0:T(8,128)S(1)} fusion(f32[8,3]{1,0:T(8,128)S(1)} %copy.121, f32[3,48,512]{2,1,0:T(8,128)} %get-tuple-element.331, f32[8,3]{1,0:T(8,128)S(1)} %copy.120, f32[8,48,512]{2,1,0:T(8,128)S(1)} %multiply_multiply_fusion.30, f32[8]{0:T(128)S(1)} %get-tuple-element.304, s32[8]{0:T(128)S(1)} %get-tuple-element.300, ...), kind=kOutput, calls=%fused_computation.69.clone.1 | convolution fusion | flops 603058176 | bytes 2163712 | tf_op jit(solution)/shard_map/while/body/eval_jaxpr/sir,sbrj->sbij/dot_general | solution.py:157
  738.0 2.1 reshape.369
  741.5 23.0 %fusion.228 = f32[3,48,512]{2,1,0:T(8,128)S(1)} fusion(f32[8,3]{1,0:T(8,128)S(1)} %copy.121, f32[3,48,512]{2,1,0:T(8,128)} %get-tuple-element.331, f32[8,3]{1,0:T(8,128)S(1)} %copy.120, f32[8,48,512]{2,1,0:T(8,128)S(1)} %multiply_multiply_fusion.30, f32[8]{0:T(128)S(1)} %get-tuple-element.304, s32[8]{0:T(128)S(1)} %get-tuple-element.300, ...), kind=kOutput, calls=%fused_computation.69.clone.1 | convolution fusion | flops 603058176 | bytes 2163712 | tf_op jit(solution)/shard_map/while/body/eval_jaxpr/sir,sbrj->sbij/dot_general | solution.py:157
  770.4 23.0 %fusion.228 = f32[3,48,512]{2,1,0:T(8,128)S(1)} fusion(f32[8,3]{1,0:T(8,128)S(1)} %copy.121, f32[3,48,512]{2,1,0:T(8,128)} %get-tuple-element.331, f32[8,3]{1,0:T(8,128)S(1)} %copy.120, f32[8,48,512]{2,1,0:T(8,128)S(1)} %multiply_multiply_fusion.30, f32[8]{0:T(128)S(1)} %get-tuple-element.304, s32[8]{0:T(128)S(1)} %get-tuple-element.300, ...), kind=kOutput, calls=%fused_computation.69.clone.1 | convolution fusion | flops 603058176 | bytes 2163712 | tf_op jit(solution)/shard_map/while/body/eval_jaxpr/sir,sbrj->sbij/dot_general | solution.py:157
  799.3 23.0 %fusion.228 = f32[3,48,512]{2,1,0:T(8,128)S(1)} fusion(f32[8,3]{1,0:T(8,128)S(1)} %copy.121, f32[3,48,512]{2,1,0:T(8,128)} %get-tuple-element.331, f32[8,3]{1,0:T(8,128)S(1)} %copy.120, f32[8,48,512]{2,1,0:T(8,128)S(1)} %multiply_multiply_fusion.30, f32[8]{0:T(128)S(1)} %get-tuple-element.304, s32[8]{0:T(128)S(1)} %get-tuple-element.300, ...), kind=kOutput, calls=%fused_computation.69.clone.1 | convolution fusion | flops 603058176 | bytes 2163712 | tf_op jit(solution)/shard_map/while/body/eval_jaxpr/sir,sbrj->sbij/dot_general | solution.py:157
  824.7 2.1 reshape.369
  828.2 23.0 %fusion.228 = f32[3,48,512]{2,1,0:T(8,128)S(1)} fusion(f32[8,3]{1,0:T(8,128)S(1)} %copy.121, f32[3,48,512]{2,1,0:T(8,128)} %get-tuple-element.331, f32[8,3]{1,0:T(8,128)S(1)} %copy.120, f32[8,48,512]{2,1,0:T(8,128)S(1)} %multiply_multiply_fusion.30, f32[8]{0:T(128)S(1)} %get-tuple-element.304, s32[8]{0:T(128)S(1)} %get-tuple-element.300, ...), kind=kOutput, calls=%fused_computation.69.clone.1 | convolution fusion | flops 603058176 | bytes 2163712 | tf_op jit(solution)/shard_map/while/body/eval_jaxpr/sir,sbrj->sbij/dot_general | solution.py:157
  853.6 2.1 reshape.369
  857.1 23.0 %fusion.228 = f32[3,48,512]{2,1,0:T(8,128)S(1)} fusion(f32[8,3]{1,0:T(8,128)S(1)} %copy.121, f32[3,48,512]{2,1,0:T(8,128)} %get-tuple-element.331, f32[8,3]{1,0:T(8,128)S(1)} %copy.120, f32[8,48,512]{2,1,0:T(8,128)S(1)} %multiply_multiply_fusion.30, f32[8]{0:T(128)S(1)} %get-tuple-element.304, s32[8]{0:T(128)S(1)} %get-tuple-element.300, ...), kind=kOutput, calls=%fused_computation.69.clone.1 | convolution fusion | flops 603058176 | bytes 2163712 | tf_op jit(solution)/shard_map/while/body/eval_jaxpr/sir,sbrj->sbij/dot_general | solution.py:157
  886.0 23.0 %fusion.228 = f32[3,48,512]{2,1,0:T(8,128)S(1)} fusion(f32[8,3]{1,0:T(8,128)S(1)} %copy.121, f32[3,48,512]{2,1,0:T(8,128)} %get-tuple-element.331, f32[8,3]{1,0:T(8,128)S(1)} %copy.120, f32[8,48,512]{2,1,0:T(8,128)S(1)} %multiply_multiply_fusion.30, f32[8]{0:T(128)S(1)} %get-tuple-element.304, s32[8]{0:T(128)S(1)} %get-tuple-element.300, ...), kind=kOutput, calls=%fused_computation.69.clone.1 | convolution fusion | flops 603058176 | bytes 2163712 | tf_op jit(solution)/shard_map/while/body/eval_jaxpr/sir,sbrj->sbij/dot_general | solution.py:157
  911.6 11.2 %all_to_all.25 = bf16[4,2,3,48,128]{4,3,2,1,0:T(8,128)(2,1)S(1)} all-to-all(bf16[4,2,3,48,128]{4,3,2,1,0:T(8,128)(2,1)S(1)} %copy.101), channel_id=1, replica_groups=mesh['groups'=2,'sky'=32,'epoch'=4,'band'=2] {'epoch'}, dimensions={0} | all-to-all | bytes 589824 | tf_op jit(solution)/shard_map/all_to_all | solution.py:25
  922.9 16.4 %collective-permute-start.2 = (bf16[2,3,8,128]{3,2,1,0:T(8,128)(2,1)S(1)}, bf16[2,3,8,128]{3,2,1,0:T(8,128)(2,1)S(1)}, u32[]{:S(2)}, u32[]{:S(2)}) collective-permute-start(bf16[2,3,8,128]{3,2,1,0:T(8,128)(2,1)S(1)} %get-tuple-element.230), channel_id=1, source_target_pairs={{0,8},{8,16},{16,24},{24,32},{32,40},{40,48},{48,56},{56,64},{64,7... | collective-permute-start | bytes 36872 | tf_op jit(solution)/shard_map/ppermute | solution.py:37
  940.7 4.2 collective-permute-done.3
  945.1 55.8 %psum.14 = f32[3]{0:T(128)S(1)} all-reduce(f32[3]{0:T(128)S(1)} %fusion.204), channel_id=1, replica_groups=mesh['groups'=2,'sky'=32,'epoch'=4,'band'=2] {'sky'}, use_global_device_ids=true, to_apply=%region_11.15 | all-reduce | flops 3 | bytes 24 | tf_op jit(solution)/shard_map/psum | solution.py:62
  1000.9 8.9 psum.15
  (290 shorter events, 55.4 us)
Async XLA Ops:
  5.5 68.3 %all-to-all-start.1 = ((s32[32,2,2]{1,2,0:T(2,128)}), s32[32,2,2]{1,2,0:T(2,128)S(1)}, u32[]{:S(2)}, u32[]{:S(2)}) async-start(s32[32,2,2]{1,2,0:T(2,128)} %copy.89), calls=%async_computation.1 | async-start | bytes 65536 | tf_op jit(solution)/shard_map/all_to_all | solution.py:145
  73.8 28.0 %all-to-all-start.2 = ((bf16[32,2,5]{2,1,0:T(2,128)(2,1)}), bf16[32,2,5]{2,1,0:T(2,128)(2,1)S(1)}, u32[]{:S(2)}, u32[]{:S(2)}) async-start(bf16[32,2,5]{2,1,0:T(2,128)(2,1)} %pad_maximum_fusion), calls=%async_computation.2 | async-start | bytes 32768 | tf_op jit(solution)/shard_map/all_to_all | solution.py:54
  101.7 29.8 %all-to-all-start = ((s32[32,1,192]{2,1,0:T(1,128)}), s32[32,1,192]{2,1,0:T(1,128)S(1)}, u32[]{:S(2)}, u32[]{:S(2)}) async-start(s32[32,1,192]{2,1,0:T(1,128)} %reshape.366), calls=%async_computation | async-start | bytes 65536 | tf_op jit(solution)/shard_map/all_to_all | solution.py:147
  115.2 22.2 %copy-start.2 = (bf16[3,32,512]{2,1,0:T(8,128)(2,1)S(1)}, bf16[3,32,512]{2,1,0:T(8,128)(2,1)}, u32[]{:S(2)}) copy-start(bf16[3,32,512]{2,1,0:T(8,128)(2,1)} %param.25) | copy-start | bytes 294916
  131.5 547.6 %all-to-all-start.3 = ((bf16[32,2,3,32,512]{4,3,2,1,0:T(8,128)(2,1)}), bf16[32,2,3,32,512]{4,3,2,1,0:T(8,128)(2,1)}, u32[]{:S(2)}, u32[]{:S(2)}) async-start(bf16[32,2,3,32,512]{4,3,2,1,0:T(8,128)(2,1)} %broadcast_select_fusion), calls=%async_computation.3 | async-start | bytes 12582912 | tf_op jit(solution)/shard_map/all_to_all | solution.py:144
  137.4 523.1 %collective-permute-start = (bf16[3,8,512]{2,1,0:T(8,128)(2,1)S(1)}, bf16[3,8,512]{2,1,0:T(8,128)(2,1)S(1)}, u32[]{:S(2)}, u32[]{:S(2)}) collective-permute-start(bf16[3,8,512]{2,1,0:T(8,128)(2,1)S(1)} %get-tuple-element.228), channel_id=1, source_target_pairs={{0,8},{8,16},{16,24},{24,32},{32,40},{40,48},{48,56},{56,64},{64,7... | collective-permute-start | bytes 73736 | tf_op jit(solution)/shard_map/ppermute | solution.py:37
  140.7 532.5 %collective-permute-start.1 = (bf16[3,8,512]{2,1,0:T(8,128)(2,1)S(1)}, bf16[3,8,512]{2,1,0:T(8,128)(2,1)S(1)}, u32[]{:S(2)}, u32[]{:S(2)}) collective-permute-start(bf16[3,8,512]{2,1,0:T(8,128)(2,1)S(1)} %get-tuple-element.229), channel_id=1, source_target_pairs={{8,0},{16,8},{24,16},{32,24},{40,32},{48,40},{56,48},{64,56},{72,6... | collective-permute-start | bytes 73736 | tf_op jit(solution)/shard_map/ppermute | solution.py:39
  679.1 265.8 %copy-start.3 = (f32[3,32]{1,0:T(4,128)S(1)}, f32[3,32]{1,0:T(4,128)}, u32[]{:S(2)}) copy-start(f32[3,32]{1,0:T(4,128)} %param.26) | copy-start | bytes 1156
  683.7 23.3 %copy-start = (f32[2,3,48,512]{3,2,1,0:T(8,128)S(1)}, f32[2,3,48,512]{3,2,1,0:T(8,128)}, u32[]{:S(2)}) copy-start(f32[2,3,48,512]{3,2,1,0:T(8,128)} %get-tuple-element.316) | copy-start | bytes 1769476 | tf_op jit(solution)/shard_map/while
  707.2 0.8 copy-start.1
  712.6 23.3 %copy-start = (f32[2,3,48,512]{3,2,1,0:T(8,128)S(1)}, f32[2,3,48,512]{3,2,1,0:T(8,128)}, u32[]{:S(2)}) copy-start(f32[2,3,48,512]{3,2,1,0:T(8,128)} %get-tuple-element.316) | copy-start | bytes 1769476 | tf_op jit(solution)/shard_map/while
  736.1 0.8 copy-start.1
  741.5 23.3 %copy-start = (f32[2,3,48,512]{3,2,1,0:T(8,128)S(1)}, f32[2,3,48,512]{3,2,1,0:T(8,128)}, u32[]{:S(2)}) copy-start(f32[2,3,48,512]{3,2,1,0:T(8,128)} %get-tuple-element.316) | copy-start | bytes 1769476 | tf_op jit(solution)/shard_map/while
  765.0 0.8 copy-start.1
  770.4 23.3 %copy-start = (f32[2,3,48,512]{3,2,1,0:T(8,128)S(1)}, f32[2,3,48,512]{3,2,1,0:T(8,128)}, u32[]{:S(2)}) copy-start(f32[2,3,48,512]{3,2,1,0:T(8,128)} %get-tuple-element.316) | copy-start | bytes 1769476 | tf_op jit(solution)/shard_map/while
  793.9 0.8 copy-start.1
  799.3 23.3 %copy-start = (f32[2,3,48,512]{3,2,1,0:T(8,128)S(1)}, f32[2,3,48,512]{3,2,1,0:T(8,128)}, u32[]{:S(2)}) copy-start(f32[2,3,48,512]{3,2,1,0:T(8,128)} %get-tuple-element.316) | copy-start | bytes 1769476 | tf_op jit(solution)/shard_map/while
  822.8 0.8 copy-start.1
  828.2 23.3 %copy-start = (f32[2,3,48,512]{3,2,1,0:T(8,128)S(1)}, f32[2,3,48,512]{3,2,1,0:T(8,128)}, u32[]{:S(2)}) copy-start(f32[2,3,48,512]{3,2,1,0:T(8,128)} %get-tuple-element.316) | copy-start | bytes 1769476 | tf_op jit(solution)/shard_map/while
  851.7 0.8 copy-start.1
  857.1 23.3 %copy-start = (f32[2,3,48,512]{3,2,1,0:T(8,128)S(1)}, f32[2,3,48,512]{3,2,1,0:T(8,128)}, u32[]{:S(2)}) copy-start(f32[2,3,48,512]{3,2,1,0:T(8,128)} %get-tuple-element.316) | copy-start | bytes 1769476 | tf_op jit(solution)/shard_map/while
  880.6 0.8 copy-start.1
  886.0 23.3 %copy-start = (f32[2,3,48,512]{3,2,1,0:T(8,128)S(1)}, f32[2,3,48,512]{3,2,1,0:T(8,128)}, u32[]{:S(2)}) copy-start(f32[2,3,48,512]{3,2,1,0:T(8,128)} %get-tuple-element.316) | copy-start | bytes 1769476 | tf_op jit(solution)/shard_map/while
  909.5 0.8 copy-start.1
  922.9 17.8 %collective-permute-start.2 = (bf16[2,3,8,128]{3,2,1,0:T(8,128)(2,1)S(1)}, bf16[2,3,8,128]{3,2,1,0:T(8,128)(2,1)S(1)}, u32[]{:S(2)}, u32[]{:S(2)}) collective-permute-start(bf16[2,3,8,128]{3,2,1,0:T(8,128)(2,1)S(1)} %get-tuple-element.230), channel_id=1, source_target_pairs={{0,8},{8,16},{16,24},{24,32},{32,40},{40,48},{48,56},{56,64},{64,7... | collective-permute-start | bytes 36872 | tf_op jit(solution)/shard_map/ppermute | solution.py:37
  939.3 5.6 collective-permute-start.3
where the time goes:
time: 1010 us
  waiting for transfers between devices  585 us (58%)
  matrix products  184 us (18%)
  starting transfers between devices  87.5 us (9%)
  blocking collectives  76 us (8%)
  local copies, waits for them, and re-layouts  42.7 us (4%)
  other arithmetic  32.6 us (3%)
    ppermute x2, waiting for transfers between devices, padded(): lax.ppermute(tail, axis, [(i, (i + 1) % count) for i in range(ends)])  518 us
    dot_general x8, matrix products, accumulate(): jnp.einsum('sir,sbrj->sbij', row_table, columns, preferred_element_type=j...  184 us
    psum x2, blocking collectives, one_axis_at_a_time(): return functools.reduce(lax.psum, axes, shard)  64.7 us
    all_to_all x1, starting transfers between devices, on_device(): lax.all_to_all(pack(slot_offset), 'sky', split_axis=0, concat_axis=0, til...  45.8 us
  transfers between devices with their start and end apart: 8, of which 7 were waited for; matrix products, arithmetic and copies ran while one was open for 2% of the time, Pallas kernels for 0%

commit v1 on v0

v1 whole, which is shorter than its diff:
```python
import functools
import math

import jax
import jax.numpy as jnp
from jax import lax
from jax.experimental import pallas as pl
from jax.experimental.pallas import tpu as pltpu
from jax.sharding import PartitionSpec as P

MESH = pl.DeviceIdType.MESH
MARGIN = 8
CLIP_WIDTH = 3.0
TAPS = tuple(range(-2, 4))
EDGE = 8
BLOCK = 32
LANES = 128


def iota(shape, dim):
    return lax.broadcasted_iota(jnp.int32, shape, dim)


def tap_values(fraction):
    sin_whole = jnp.sin(math.pi * fraction)
    sin_third = jnp.sin((math.pi / 3.0) * fraction)
    cos_third = jnp.cos((math.pi / 3.0) * fraction)
    values = []
    for d in TAPS:
        u = d - fraction
        top = -math.cos(math.pi * d) * sin_whole
        third = math.sin(math.pi * d / 3.0) * cos_third - math.cos(math.pi * d / 3.0) * sin_third
        value = top * third / ((math.pi * math.pi / 3.0) * u * u)
        value = jnp.where(jnp.abs(u) < 3.0, value, 0.0)
        values.append(value.astype(jnp.bfloat16).astype(jnp.float32))
    return values


def tap_select(gap, taps):
    value = jnp.zeros(gap.shape, jnp.float32)
    for d, tap in zip(TAPS, taps):
        value = jnp.where(gap == d, tap, value)
    return value


def greet(peers):
    barrier = pltpu.get_barrier_semaphore()
    for peer in peers:
        pl.semaphore_signal(barrier, inc=1, device_id=peer, device_id_type=MESH)
    pl.semaphore_wait(barrier, len(peers))


def places(n, ne):
    me = lax.axis_index("sky")
    e = lax.axis_index("epoch")

    def sky(shift):
        return lax.rem(me + shift + n, n)

    def epoch(shift):
        return lax.rem(e + shift + ne, ne)

    return sky, epoch


def remote(src, dst, send_sem, recv_sem, peer):
    return pltpu.make_async_remote_copy(
        src_ref=src, dst_ref=dst, send_sem=send_sem, recv_sem=recv_sem, device_id=peer, device_id_type=MESH
    )


def gather_kernel(
    n, ne, offset, pix_hbm, frac_ref, sigma_ref, mask_ref, tmpl_hbm, warped_hbm, cover_hbm, mc_hbm, all_hbm,
    pix, warped, cover, mc, held, kx, taps, squares,
    in_sem, chain_send, chain_recv, fan_send, fan_recv, x_send, x_recv, out_sem, slot_sem, mc_sem,
):
    slots, lines, width = pix.shape
    bands, rows = held.shape[2], held.shape[3]
    canvas = rows + 2 * MARGIN
    steps = n // 4
    per_step = slots // steps
    sky, epoch = places(n, ne)
    me = sky(0)
    load_pix = pltpu.make_async_copy(pix_hbm, pix, in_sem.at[0])

    def load_own(q):
        return pltpu.make_async_copy(
            tmpl_hbm.at[:, :, pl.ds(q * LANES, LANES)], held.at[me, q], in_sem.at[1 + q]
        )

    for q in range(ne):
        load_own(q).start()
    load_pix.start()
    greet([{"sky": sky(k)} for k in (-2, -1, 1, 2)] + [{"epoch": epoch(k)} for k in (-1, 1)])
    for q in range(ne):
        load_own(q).wait()

    def quarter(c):
        return epoch(c)

    def block(side, distance):
        return sky(-distance if side == 0 else distance)

    def chain(side, j, c):
        piece = held.at[block(side, 2 * j), quarter(c)]
        return remote(
            piece, piece, chain_send.at[side, j, c], chain_recv.at[side, j, c],
            {"sky": sky(2 if side == 0 else -2)},
        )

    def fan(side, j, c):
        piece = held.at[block(side, 2 * j), quarter(c)]
        return remote(
            piece, piece, fan_send.at[side, j, c], fan_recv.at[side, j, c],
            {"sky": sky(1 if side == 0 else -1)},
        )

    def across(owner, c):
        piece = held.at[owner, quarter(c)]
        return remote(
            piece, piece, x_send.at[c, owner], x_recv.at[c, owner], {"epoch": epoch(1 if c == 0 else -1)}
        )

    for c in (0, 1):
        for side in (0, 1):
            chain(side, 0, c).start()
    for c in (0, 1):
        for side in (0, 1):
            fan(side, 0, c).start()

    lanes = mc.shape[2]
    lane = iota((16, lanes), 1)
    tail = lane - width
    inner = lax.rem(tail, 32)
    chosen = jnp.where(
        tail < 0,
        lane // BLOCK,
        jnp.where(inner < 16, inner, jnp.where(inner < 24, 0, 15)),
    )
    spread = jnp.where((chosen == iota((16, lanes), 0)) & (tail < bands * 32), 1.0, 0.0).astype(jnp.bfloat16)
    kx[...] = jnp.zeros_like(kx)
    fractions = frac_ref[...].astype(jnp.float32)
    for axis in (0, 1):
        wide = jnp.broadcast_to(fractions[:, axis : axis + 1], (slots, LANES))
        for i, value in enumerate(tap_values(wide)):
            taps[axis * len(TAPS) + i] = value
    sigma = sigma_ref[...].astype(jnp.float32)
    band_of = iota((slots, LANES), 1) // 32
    square = jnp.zeros((slots, LANES), jnp.float32)
    for b in range(bands):
        s = jnp.broadcast_to(sigma[:, b : b + 1], (slots, LANES))
        square = jnp.where(band_of == b, 1.0 / (s * s), square)
    squares[...] = square
    load_pix.wait()
    ones = jnp.ones((rows, LANES), jnp.bfloat16)

    def warp(slot, table):
        dy = offset[slot, 0]
        dx = offset[slot, 1]
        row_taps = [taps[i, pl.ds(slot, 1), :] for i in range(6)]
        col_taps = [taps[6 + i, pl.ds(slot, 1), :] for i in range(6)]
        lead = (LANES, LANES)
        middle = tap_select(iota(lead, 1) - iota(lead, 0) - dx, col_taps).astype(jnp.bfloat16)
        rim = (16, LANES)
        gap = iota(rim, 1) - iota(rim, 0) - dx
        above = tap_select(gap + 16, col_taps).astype(jnp.bfloat16)
        below = tap_select(gap - LANES, col_taps).astype(jnp.bfloat16)
        blocks = width // LANES
        for jb in range(blocks):
            span = slice(jb * LANES, (jb + 1) * LANES)
            table[span, span] = middle
            if jb > 0:
                table[jb * LANES - 16 : jb * LANES, span] = above
            if jb < blocks - 1:
                table[(jb + 1) * LANES : (jb + 1) * LANES + 16, span] = below
        columns = jnp.dot(pix[slot], table[...], preferred_element_type=jnp.float32).astype(jnp.bfloat16)
        shape = (canvas, LANES)
        gap = iota(shape, 0) - MARGIN - dy - iota(shape, 1)
        row_table = tap_select(gap, row_taps)[:, :rows].astype(jnp.bfloat16)
        for b in range(bands):
            warped[slot, b * canvas : (b + 1) * canvas] = jnp.dot(
                row_table, columns[b * rows : (b + 1) * rows], preferred_element_type=jnp.float32
            ).astype(jnp.bfloat16)
        cover[slot] = jnp.clip(jnp.dot(row_table, ones, preferred_element_type=jnp.float32), 0.0, 1.0)
        shape = (8, lanes)
        at = iota(shape, 1)
        over = at - width
        part = lax.rem(over, 32)
        column = jnp.where(
            over < 0,
            at,
            jnp.where(part < 16, 256, jnp.where(part < 24, part - 16, width - 32 + part)),
        )
        col_cover = jnp.zeros(shape, jnp.float32)
        for d, tap in zip(TAPS, col_taps):
            source = column - dx - d
            tap = jnp.concatenate([tap] * (lanes // LANES), axis=1)
            col_cover = col_cover + jnp.where((source >= 0) & (source < width), tap, 0.0)
        col_cover = jnp.clip(col_cover, 0.0, 1.0)
        mask_rows = mask_ref.shape[1]
        mask = mask_ref[slot].astype(jnp.float32).astype(jnp.bfloat16)
        planes = jnp.dot(mask, spread, preferred_element_type=jnp.float32) * col_cover[:mask_rows]
        mc[slot, 0:mask_rows, 0:width] = planes[:, :width]
        mc[slot, 0:mask_rows, width:] = planes[:, width:] * squares[pl.ds(slot, 1), :]

    def store_out(owner):
        return pltpu.make_async_copy(held.at[owner], all_hbm.at[owner], out_sem.at[owner])

    def slots_out(step):
        which = pl.ds(step * per_step, per_step)
        return (
            pltpu.make_async_copy(warped.at[which], warped_hbm.at[which], slot_sem.at[0, step]),
            pltpu.make_async_copy(cover.at[which], cover_hbm.at[which], slot_sem.at[1, step]),
        )

    def body(j, stage):
        for c in (0, 1):
            chain(0, j - 1, c).wait_recv()
            if stage < 2:
                chain(0, j, c).start()
                chain(1, j - 1, c).wait_recv()
            if stage < 1:
                chain(1, j, c).start()
            if stage < 2:
                for side in (0, 1):
                    fan(side, j, c).start()
            across(block(0, 2 * j), c).start()
            if stage < 2:
                across(block(1, 2 * j), c).start()
        for c in (0, 1):
            for side in (0, 1):
                fan(side, j - 1, c).wait_recv()
                across(block(side, 2 * j - 1), c).start()

        @pl.loop((j - 1) * per_step, j * per_step)
        def _(slot):
            warp(slot, kx)

        for copy in slots_out(j - 1):
            copy.start()

    @pl.loop(1, steps - 1)
    def _(j):
        body(j, 0)

    body(steps - 1, 1)
    body(steps, 2)
    mc_out = pltpu.make_async_copy(mc, mc_hbm, mc_sem.at[0])
    mc_out.start()
    store_out(me).start()

    @pl.loop(1, n)
    def _(k):
        owner = sky(k)
        for c in (0, 1):
            across(owner, c).wait_recv()
        store_out(owner).start()

    @pl.loop(1, n)
    def _(k):
        owner = sky(k)
        for c in (0, 1):
            across(owner, c).wait_send()
        store_out(owner).wait()

    store_out(me).wait()

    @pl.loop(0, steps)
    def _(j):
        for c in (0, 1):
            chain(0, j, c).wait_send()
            for side in (0, 1):
                fan(side, j, c).wait_send()
        for copy in slots_out(j):
            copy.wait()

    @pl.loop(0, steps - 1)
    def _(j):
        for c in (0, 1):
            chain(1, j, c).wait_send()

    mc_out.wait()


def accumulate_kernel(
    ne, tile, count, warped_hbm, cover_hbm, mc_hbm, all_hbm, sigma_ref, prior_ref, part_hbm, wpart_hbm, total_ref,
    warped, cover, mc, tmpl, framed, flux, wsum, wout, scales, slot_sem, sem,
):
    slots, width = warped.shape[0], warped.shape[2]
    n, quarters, bands, rows = tmpl.shape[:4]
    canvas = rows + 2 * MARGIN
    pieces = slot_sem.shape[1]
    piece = slots // pieces
    load_tmpl = pltpu.make_async_copy(all_hbm, tmpl, sem.at[0])
    load_mc = pltpu.make_async_copy(mc_hbm, mc, sem.at[1])

    def load_slots(q):
        which = pl.ds(q * piece, piece)
        return (
            pltpu.make_async_copy(warped_hbm.at[which], warped.at[which], slot_sem.at[0, q]),
            pltpu.make_async_copy(cover_hbm.at[which], cover.at[which], slot_sem.at[1, q]),
        )

    load_tmpl.start()
    load_mc.start()
    for q in range(pieces):
        for copy in load_slots(q):
            copy.start()

    sigma = sigma_ref[...].astype(jnp.float32)
    for b in range(bands):
        s = jnp.broadcast_to(sigma[:, b : b + 1], (slots, LANES))
        scales[b] = CLIP_WIDTH * s
        scales[bands + b] = 1.0 / (CLIP_WIDTH * s)
        scales[2 * bands + b] = 1.0 / (s * s)

    @pl.loop(0, n)
    def _(t):
        at = pl.ds(pl.multiple_of(t * rows, rows), rows)
        for b in range(bands):
            flux[b, at, :] = jnp.zeros((rows, width), jnp.float32)
        wsum[at, :] = jnp.zeros((rows, LANES), jnp.float32)

    total_rows = flux.shape[1]
    ends = total_rows - n * rows
    for b in range(bands):
        flux[b, n * rows :, :] = jnp.zeros((ends, width), jnp.float32)
        framed[b, 0:MARGIN, :] = jnp.zeros((MARGIN, width), jnp.float32)
        framed[b, total_rows - MARGIN :, :] = jnp.zeros((MARGIN, width), jnp.float32)
    wsum[n * rows :, :] = jnp.zeros((ends, LANES), jnp.float32)
    load_tmpl.wait()

    @pl.loop(0, n)
    def _(t):
        at = pl.ds(pl.multiple_of(t * rows + MARGIN, MARGIN), rows)
        for b in range(bands):
            for q in range(quarters):
                framed[b, at, q * LANES : (q + 1) * LANES] = tmpl[t, q, b].astype(jnp.float32)

    load_mc.wait()
    live = count[0]
    mask_rows = canvas // 8

    def spread(block):
        wide = block.shape[1]
        return jnp.broadcast_to(block[:, None, :], (mask_rows, 8, wide)).reshape(canvas, wide)

    def one(p):
        row0 = pl.multiple_of(tile[p, 0] * rows, rows)
        at = pl.ds(row0, canvas)
        rim = cover[p]
        scale = [scales[i, pl.ds(p, 1), :] for i in range(3 * bands)]
        for q in range(width // LANES):
            span = pl.ds(q * LANES, LANES)
            plane = spread(mc[p, 0:mask_rows, span]) * rim
            for b in range(bands):
                frame = framed[b, at, span]
                moved = warped[p, pl.ds(b * canvas, canvas), span].astype(jnp.float32)
                moved = jnp.tanh((moved - frame) * scale[bands + b])
                flux[b, at, span] += (plane * scale[2 * bands + b]) * (frame + scale[b] * moved)
        wsum[at, :] += spread(mc[p, 0:mask_rows, pl.ds(width, LANES)]) * rim

    for q in range(pieces):
        for copy in load_slots(q):
            copy.wait()

        @pl.loop(q * piece, jnp.minimum(live, (q + 1) * piece))
        def _(p):
            one(p)

    def add_rows(t, total):
        at = pl.ds(pl.multiple_of(t * rows + MARGIN, MARGIN), rows)
        block = wsum[at, :]
        for g in range(ne):
            wout[g, t] = block[g * 8 : (g + 1) * 8]
        for b in range(bands):
            for q in range(quarters):
                tmpl[t, q, b] = flux[b, at, q * LANES : (q + 1) * LANES].astype(jnp.bfloat16)
        return total + sum(block[i : i + 8] for i in range(0, rows, 8))

    total = lax.fori_loop(0, n, add_rows, jnp.zeros((8, LANES), jnp.float32))
    part_out = pltpu.make_async_copy(tmpl, part_hbm, sem.at[0])
    part_out.start()
    w_out = pltpu.make_async_copy(wout, wpart_hbm, sem.at[1])
    w_out.start()
    lane = iota((8, LANES), 1)
    inner = lax.rem(lane, 32)
    times = jnp.where(
        lane >= bands * 32,
        0.0,
        jnp.where(
            inner >= 16,
            1.0,
            jnp.where((inner == 0) | (inner == 15), float(BLOCK - EDGE), float(BLOCK)),
        ),
    )
    total = jnp.broadcast_to(jnp.sum(total, axis=0, keepdims=True), (8, LANES)) * times
    for b in range(bands):
        prior = jnp.sum(prior_ref[b : b + 1, :], axis=1, keepdims=True) * (width / ne)
        total = total + jnp.where(lane == b * 32, prior, 0.0)
    total_ref[...] = total
    part_out.wait()
    w_out.wait()


def reduce_kernel(
    n, ne, part_hbm, wpart_hbm, total_ref, tmpl_ref, prior_ref, image_ref, norm_ref,
    part, wpart, xin, xwin, xtin, shared, chain_out, wchain_out, chain_in, wchain_in,
    fan_out, wfan_out, fan_in, wfan_in, half_out, half_in, kept,
    load_sem, x_send, x_recv, xw_sem, xt_sem, chain_send, chain_recv, fan_send, fan_recv, half_sem, kept_sem,
):
    bands, rows = part.shape[2:4]
    width = ne * LANES
    steps = n // 4
    sky, epoch = places(n, ne)
    e = epoch(0)

    def step_owners(s):
        i = steps - s
        return (sky(2 * i), sky(-2 * i), sky(2 * i - 1), sky(1 - 2 * i))

    def load(c):
        return pltpu.make_async_copy(part_hbm.at[:, epoch(c)], part.at[c], load_sem.at[c])

    load_w = pltpu.make_async_copy(wpart_hbm.at[e], wpart, load_sem.at[2])
    for c in (0, 1):
        load(c).start()
    load_w.start()
    greet([{"sky": sky(k)} for k in (-2, -1, 1, 2)] + [{"epoch": epoch(k)} for k in range(1, ne)])

    def cross(owner, c):
        return remote(
            part_hbm.at[owner, epoch(-1 if c == 0 else 2)],
            xin.at[c, owner],
            x_send.at[c, owner],
            x_recv.at[c, owner],
            {"epoch": epoch(-1 if c == 0 else 1)},
        )

    def cross_w(k):
        peer = epoch(k)
        return remote(
            wpart_hbm.at[peer], xwin.at[k - 1], xw_sem.at[0, k - 1], xw_sem.at[1, k - 1], {"epoch": peer}
        )

    def cross_t(k):
        return remote(
            total_ref, xtin.at[k - 1], xt_sem.at[0, k - 1], xt_sem.at[1, k - 1], {"epoch": epoch(k)}
        )

    def cross_owners(owners):
        for owner in owners:
            for c in (0, 1):
                cross(owner, c).start()

    first = step_owners(0)
    cross_owners((first[0], first[2], first[3]))
    for k in range(1, ne):
        cross_t(k).start()
        cross_w(k).start()

    @pl.loop(1, steps)
    def _(s):
        cross_owners(step_owners(s))

    cross_owners((sky(0),))

    def chain(side, s, c):
        whole = c < 2
        return remote(
            chain_out.at[side, s, c] if whole else wchain_out.at[side, s],
            chain_in.at[side, s, c] if whole else wchain_in.at[side, s],
            chain_send.at[side, s, c],
            chain_recv.at[side, s, c],
            {"sky": sky(2 if side == 0 else -2)},
        )

    def fan(side, k, c):
        whole = c < 2
        return remote(
            fan_out.at[side, k, c] if whole else wfan_out.at[side, k],
            fan_in.at[side, k, c] if whole else wfan_in.at[side, k],
            fan_send.at[side, k, c],
            fan_recv.at[side, k, c],
            {"sky": sky(1 if side == 0 else -1)},
        )

    def own(owner, c):
        if c < 2:
            return part[c, owner].astype(jnp.float32) + xin[c, owner].astype(jnp.float32)
        block = wpart[owner]
        for k in range(1, ne):
            block = block + xwin[k - 1, owner]
        return jnp.concatenate([block, shared[...]], axis=0)

    def received(kind, side, k, c):
        if c < 2:
            return (chain_in if kind == 0 else fan_in)[side, k, c].astype(jnp.float32)
        return (wchain_in if kind == 0 else wfan_in)[side, k]

    def wait_cross(owner):
        for c in (0, 1):
            cross(owner, c).wait_recv()

    def chain_step(s, side, has_chain, has_fan):
        i = steps - s
        owner = sky(2 * i if side == 0 else -2 * i)
        for c in range(3):
            if has_chain:
                chain(side, s - 1, c).wait_recv()
            if has_fan:
                fan(side, i, c).wait_recv()
            value = own(owner, c)
            if has_chain:
                value = value + received(0, side, s - 1, c)
            if has_fan:
                value = value + received(1, side, i, c)
            if c < 2:
                chain_out[side, s, c] = value.astype(jnp.bfloat16)
            else:
                wchain_out[side, s] = value
            chain(side, s, c).start()

    def fan_step(s, side):
        k = steps - s - 1
        owner = sky(2 * k + 1 if side == 0 else -2 * k - 1)
        wait_cross(owner)
        for c in range(3):
            value = own(owner, c)
            if c < 2:
                fan_out[side, k, c] = value.astype(jnp.bfloat16)
            else:
                wfan_out[side, k] = value
            fan(side, k, c).start()

    for c in (0, 1):
        load(c).wait()
    load_w.wait()
    for k in range(1, ne):
        cross_t(k).wait_recv()
        cross_w(k).wait_recv()
    gathered = total_ref[...]
    for k in range(1, ne):
        gathered = gathered + xtin[k - 1]
    shared[...] = gathered

    wait_cross(first[0])
    chain_step(0, 0, False, False)
    for side in (0, 1):
        fan_step(0, side)
    for side in (0, 1):
        wait_cross(sky(2 * (steps - 1) if side == 0 else -2 * (steps - 1)))
        chain_step(1, side, side == 0, True)
    for side in (0, 1):
        fan_step(1, side)

    @pl.loop(2, steps)
    def _(s):
        i = steps - s
        for side in (0, 1):
            wait_cross(sky(2 * i if side == 0 else -2 * i))
            chain_step(s, side, True, True)
        for side in (0, 1):
            fan_step(s, side)

    me = sky(0)
    wait_cross(me)
    sums = []
    for c in (1, 2, 0):
        value = own(me, c)
        for side in (0, 1):
            fan(side, 0, c).wait_recv()
            value = value + received(1, side, 0, c)
        for side in (0, 1):
            chain(side, steps - 1, c).wait_recv()
            value = value + received(0, side, steps - 1, c)
        if c == 1:
            half_out[...] = value.astype(jnp.bfloat16)
            half = remote(half_out, half_in, half_sem.at[0], half_sem.at[1], {"epoch": epoch(1)})
            half.start()
        elif c == 2:
            kept[e] = value[0:8]
            total = value[8:9]

            def keep(k):
                return remote(
                    kept.at[e], kept.at[e], kept_sem.at[0, k - 1], kept_sem.at[1, k - 1], {"epoch": epoch(k)}
                )

            for k in range(1, ne):
                keep(k).start()
        else:
            mine = value

    lane = iota((LANES, LANES), 1) + e * LANES
    row = iota((LANES, LANES), 0)
    inner = jnp.where(
        lane < EDGE, 16 + lane, jnp.where(lane >= width - EDGE, lane - (width - 32), lane // BLOCK)
    )
    here = pl.ds(pl.multiple_of(e * LANES, LANES), LANES)
    lane1 = iota((1, LANES), 1)
    eye = iota((rows, rows), 0) == iota((rows, rows), 1)
    half.wait()
    for k in range(1, ne):
        keep(k).wait()
    weights = kept[...].reshape(rows, LANES)
    for b in range(bands):
        pick = jnp.where(row == inner + b * 32, 1.0, 0.0)
        weight = jnp.dot(
            weights, pick, preferred_element_type=jnp.float32, precision=lax.Precision.HIGHEST
        )
        prior = jnp.sum(
            jnp.where(eye, jnp.broadcast_to(prior_ref[b : b + 1, :], (rows, rows)), 0.0), axis=1, keepdims=True
        )
        depth = weight + prior
        base = tmpl_ref[b, :, here].astype(jnp.float32)
        image_ref[b] = (mine[b] + half_in[b].astype(jnp.float32) + prior * base) / depth
        band = jnp.sum(jnp.where(lane1 // 32 == b, total, 0.0), axis=1, keepdims=True)
        norm_ref[b] = depth / (band / float(rows * n * width))

    @pl.loop(0, n)
    def _(k):
        for c in (0, 1):
            cross(sky(k), c).wait_send()

    for k in range(1, ne):
        cross_w(k).wait_send()
        cross_t(k).wait_send()

    @pl.loop(0, steps)
    def _(s):
        for c in range(3):
            chain(0, s, c).wait_send()
            for side in (0, 1):
                fan(side, s, c).wait_send()

    @pl.loop(1, steps)
    def _(s):
        for c in range(3):
            chain(1, s, c).wait_send()


def on_device(
    slot_pixels,
    slot_tile,
    slot_offset,
    slot_frac,
    slot_sigma,
    clip_mask,
    slot_count,
    template,
    prior_weight,
):
    n = lax.axis_size("sky")
    ne = lax.axis_size("epoch")
    steps = n // 4
    slots, bands, rows, width = slot_pixels.shape
    canvas = rows + 2 * MARGIN
    lanes = width + LANES
    smem = pl.BlockSpec(memory_space=pltpu.SMEM)
    vmem = pl.BlockSpec(memory_space=pltpu.VMEM)
    hbm = pl.BlockSpec(memory_space=pl.ANY)
    dma = pltpu.SemaphoreType.DMA
    bf16, f32 = jnp.bfloat16, jnp.float32
    warped_type = jax.ShapeDtypeStruct((slots, bands * canvas, width), bf16)
    cover_type = jax.ShapeDtypeStruct((slots, canvas, LANES), f32)
    mc_type = jax.ShapeDtypeStruct((slots, 8, lanes), f32)
    blocks_type = jax.ShapeDtypeStruct((n, ne, bands, rows, LANES), bf16)

    def like(shape):
        return pltpu.VMEM(shape.shape, shape.dtype)

    warped, cover, mc, gathered = pl.pallas_call(
        functools.partial(gather_kernel, n, ne),
        out_shape=(warped_type, cover_type, mc_type, blocks_type),
        in_specs=[smem, hbm, vmem, vmem, vmem, hbm],
        out_specs=(hbm, hbm, hbm, hbm),
        scratch_shapes=[
            pltpu.VMEM((slots, bands * rows, width), bf16),
            like(warped_type),
            like(cover_type),
            like(mc_type),
            like(blocks_type),
            pltpu.VMEM((width, width), bf16),
            pltpu.VMEM((2 * len(TAPS), slots, LANES), f32),
            pltpu.VMEM((slots, LANES), f32),
            dma((1 + ne,)),
            dma((2, steps, 2)),
            dma((2, steps, 2)),
            dma((2, steps, 2)),
            dma((2, steps, 2)),
            dma((2, n)),
            dma((2, n)),
            dma((n,)),
            dma((2, steps)),
            dma((1,)),
        ],
        compiler_params=pltpu.CompilerParams(collective_id=0, has_side_effects=True),
        name="gather",
    )(slot_offset, slot_pixels.reshape(slots, bands * rows, width), slot_frac, slot_sigma, clip_mask, template)

    padded = n * rows + 2 * MARGIN
    wpart_type = jax.ShapeDtypeStruct((ne, n, 8, LANES), f32)
    total_type = jax.ShapeDtypeStruct((8, LANES), f32)
    part, wpart, total = pl.pallas_call(
        functools.partial(accumulate_kernel, ne),
        out_shape=(blocks_type, wpart_type, total_type),
        in_specs=[smem, smem, hbm, hbm, hbm, hbm, vmem, vmem],
        out_specs=(hbm, hbm, vmem),
        scratch_shapes=[
            like(warped_type),
            like(cover_type),
            like(mc_type),
            like(blocks_type),
            pltpu.VMEM((bands, padded, width), f32),
            pltpu.VMEM((bands, padded, width), f32),
            pltpu.VMEM((padded, LANES), f32),
            like(wpart_type),
            pltpu.VMEM((3 * bands, slots, LANES), f32),
            dma((2, 6)),
            dma((2,)),
        ],
        name="accumulate",
    )(slot_tile, slot_count, warped, cover, mc, gathered, slot_sigma, prior_weight)

    half_type = (bands, rows, LANES)
    out = jax.ShapeDtypeStruct((bands, rows, width // ne), f32)
    image, norm = pl.pallas_call(
        functools.partial(reduce_kernel, n, ne),
        out_shape=(out, out),
        in_specs=[hbm, hbm, vmem, vmem, vmem],
        out_specs=(vmem, vmem),
        scratch_shapes=[
            pltpu.VMEM((2, n) + half_type, bf16),
            pltpu.VMEM((n, 8, LANES), f32),
            pltpu.VMEM((2, n) + half_type, bf16),
            pltpu.VMEM((ne - 1, n, 8, LANES), f32),
            pltpu.VMEM((ne - 1, 8, LANES), f32),
            pltpu.VMEM((8, LANES), f32),
            pltpu.VMEM((2, steps, 2) + half_type, bf16),
            pltpu.VMEM((2, steps, 16, LANES), f32),
            pltpu.VMEM((2, steps, 2) + half_type, bf16),
            pltpu.VMEM((2, steps, 16, LANES), f32),
            pltpu.VMEM((2, steps, 2) + half_type, bf16),
            pltpu.VMEM((2, steps, 16, LANES), f32),
            pltpu.VMEM((2, steps, 2) + half_type, bf16),
            pltpu.VMEM((2, steps, 16, LANES), f32),
            pltpu.VMEM(half_type, bf16),
            pltpu.VMEM(half_type, bf16),
            pltpu.VMEM((ne, 8, LANES), f32),
            dma((3,)),
            dma((2, n)),
            dma((2, n)),
            dma((2, ne - 1)),
            dma((2, ne - 1)),
            dma((2, steps, 3)),
            dma((2, steps, 3)),
            dma((2, steps, 3)),
            dma((2, steps, 3)),
            dma((2,)),
            dma((2, ne - 1)),
        ],
        compiler_params=pltpu.CompilerParams(collective_id=1, has_side_effects=True),
        name="reduce",
    )(part, wpart, total, template, prior_weight)
    return (image.astype(bf16), norm.astype(bf16))


def solution(mesh):
    in_specs = (
        P(("groups", "sky", "epoch"), "band", None, None),
        P(("groups", "sky", "epoch"), None),
        P(("groups", "sky", "epoch"), None),
        P(("groups", "sky", "epoch"), None),
        P(("groups", "sky", "epoch"), "band"),
        P(("groups", "sky", "epoch"), None, None),
        P(("groups", "sky", "epoch")),
        P("band", ("groups", "sky"), None),
        P("band", ("groups", "sky")),
    )
    out_specs = (P("band", ("groups", "sky"), "epoch"), P("band", ("groups", "sky"), "epoch"))
    return jax.shard_map(
        on_device, mesh=mesh, in_specs=in_specs, out_specs=out_specs, check_vma=False
    )
```

time: 1010 us -> 178 us (0.18)
  waiting for transfers between devices: 585 us -> 0 us
  matrix products: 184 us -> 0 us
  Pallas kernels: 0 us -> 166 us
  starting transfers between devices: 87.5 us -> 0 us
  blocking collectives: 76 us -> 0 us
  local copies, waits for them, and re-layouts: 42.7 us -> 7.04 us
  other arithmetic: 32.6 us -> 2.82 us
    ppermute x4 -> x0, waiting for transfers between devices: 535 us -> none  [the longest x2 518 us: padded(): lax.ppermute(tail, axis, [(i, (i + 1) % count) for i in range(ends)])]
    dot_general x8 -> x0, matrix products: 184 us -> none  [accumulate(): jnp.einsum('sir,sbrj->sbij', row_table, columns, preferred_element_type=j...]
    pallas_call x0 -> x3, Pallas kernels: none -> 166 us  [the longest x1 89.3 us: on_device(): pl.pallas_call(functools.partial(gather_kernel, n, ne), out_shape=(warped...]
    all_to_all x4 -> x0, starting transfers between devices: 65.3 us -> none  [the longest x1 45.8 us: on_device(): lax.all_to_all(pack(slot_offset), 'sky', split_axis=0, concat_axis=0, til...]
    psum x2 -> x0, blocking collectives: 64.7 us -> none  [one_axis_at_a_time(): return functools.reduce(lax.psum, axes, shard)]
    all_to_all x4 -> x0, waiting for transfers between devices: 50.4 us -> none  [the longest x1 16.3 us: on_device(): lax.all_to_all(packed_mask, 'sky', split_axis=0, concat_axis=0, tiled=True)]
    ppermute x4 -> x0, starting transfers between devices: 22.3 us -> none  [the longest x2 19.7 us: padded(): lax.ppermute(tail, axis, [(i, (i + 1) % count) for i in range(ends)])]
    reshape x9 -> x0, local copies, waits for them, and re-layouts: 16.8 us -> none  [the longest x8 16.7 us: accumulate(): expanded = expanded.reshape(block_slots, canvas_rows, tile_cols)]
  transfers between devices with their start and end apart: 8 -> 0, of which waited for: 7 -> 0; matrix products, arithmetic and copies ran while one was open for 2% -> 0% of each run, Pallas kernels for 0% -> 0%
where the time goes in v1:
time: 178 us; the launch traced here: 177 us
  Pallas kernels  166 us (93%)
  local copies, waits for them, and re-layouts  7.04 us (4%)
  other arithmetic  2.82 us (2%)
    pallas_call x1, Pallas kernels, on_device(): pl.pallas_call(functools.partial(gather_kernel, n, ne), out_shape=(warped...  89.3 us
    pallas_call x1, Pallas kernels, on_device(): pl.pallas_call(functools.partial(reduce_kernel, n, ne), out_shape=(out, o...  63.3 us
    pallas_call x1, Pallas kernels, on_device(): pl.pallas_call(functools.partial(accumulate_kernel, ne), out_shape=(block...  13.5 us
    unnamed x5, local copies, waits for them, and re-layouts  7.04 us

profile of v1, /device:TPU:40, one launch (start us, length us, event | category | flops | bytes accessed | tf_op | source)
XLA Modules:
  0.0 177.2 jit_solution(709290904345582239)
XLA Ops:
  1.3 1.4 copy.13.sigma_ref
  2.6 1.3 copy.12.frac_ref
  4.0 1.3 copy.15.tile
  5.3 1.4 copy.11.offset
  6.7 1.6 copy.14.mask_ref
  8.3 89.3 %gather.1 = (bf16[48,144,512]{2,1,0:T(8,128)(2,1)}, f32[48,48,128]{2,1,0:T(8,128)}, f32[48,8,640]{2,1,0:T(8,128)}, bf16[32,4,3,32,128]{4,3,2,1,0:T(8,128)(2,1)}) custom-call(s32[48,2]{1,0:T(8,128)} %copy.11.offset, bf16[48,96,512]{2,1,0:T(8,128)(2,1)} %bitcast.1, bf16[48,2]{1,0:T(8,128)(2,1)} %copy.12.frac_ref, bf16[48,3]{1,0:T(8,128)(2,1)} %copy.13.sigma_ref, ...), custom_call_target="tpu_custom_call" | custom-call | tf_op jit(solution)/shard_map/gather/pallas_call | solution.py:673
  97.6 13.5 %accumulate.1 = (bf16[32,4,3,32,128]{4,3,2,1,0:T(8,128)(2,1)}, f32[4,32,8,128]{3,2,1,0:T(8,128)}, f32[8,128]{1,0:T(8,128)}) custom-call(s32[48,1]{1,0:T(8,128)} %copy.15.tile, s32[1]{0:T(128)S(6)} %copy.17.count, bf16[48,144,512]{2,1,0:T(8,128)(2,1)} %get-tuple-element.11.warped_hbm, f32[48,48,128]{2,1,0:T(8,128)} %get-tuple-element.12.cover_hbm, ...), custom_call_target="tpu_custom_call" | custom-call | tf_op jit(solution)/shard_map/accumulate/pallas_call | solution.py:705
  111.1 63.3 %reduce.1 = (f32[3,32,128]{2,1,0:T(8,128)}, f32[3,32,128]{2,1,0:T(8,128)}) custom-call(bf16[32,4,3,32,128]{4,3,2,1,0:T(8,128)(2,1)} %get-tuple-element.15.part_hbm, f32[4,32,8,128]{3,2,1,0:T(8,128)} %get-tuple-element.16.wpart_hbm, f32[8,128]{1,0:T(8,128)} %get-tuple-element.17.total_ref, bf16[3,32,512]{2,1,0:T(8,128)(2,1)} %tmpl_ref.1, f32[3,32]{1,0:T(4,128)} %prior_ref.3), custom_call_target="tpu_custom_call" | custom-call | tf_op jit(solution)/shard_map/reduce/pallas_call | solution.py:728
  174.4 1.4 convert_element_type.6
  175.8 1.4 convert_element_type.7
